TPU v7x, 32 devices: a whole 2x2x4 slice. The times are simulated.
32 devices in a mesh: dp: 16 (over z, y, core), mp: 2 (over x).
Axes of the slice: x: 2, y: 2, z: 4, core: 2. Of those that a mesh axis runs over, the one named last changes fastest.
Arguments:
- features: bfloat16 [768, 384], P('dp'), may hold values from -100 to 100
- teacher_weight: float32 [384, 131072], P(None, ('dp', 'mp')), may hold values from -250 to 250
- student_weight: float32 [384, 131072], P(None, ('dp', 'mp')), may hold values from -24 to 24
- center: float32 [131072], P(('dp', 'mp')), may hold values from -1 to 1
Outputs:
- blended: float32 [384, 131072], P(None, ('dp', 'mp'))
- new_center: float32 [131072], P(('dp', 'mp'))
- log_targets: float32 [768, 131072], P(None, ('dp', 'mp'))
All inputs are finite; a program needn't handle non-finite values.
Results may differ from a plain program's by a relative error of at most 0.0003.
Values may be sent and summed in bfloat16 or wider, within the bound.
A program may use at most 64 MiB of HBM per device.

v0:
```python
import jax
import jax.numpy as jnp
from jax import lax
from jax.sharding import PartitionSpec as P

ema_momentum = 0.994
center_momentum = 0.9
teacher_temp = 0.07
epsilon = 1e-06


def shards(features, teacher_weight, student_weight, center):
    blended = ema_momentum * teacher_weight + (1.0 - ema_momentum) * student_weight
    col_norm = jnp.sqrt(jnp.sum(blended * blended, axis=0, keepdims=True) + epsilon)
    protos = (blended / col_norm).astype(jnp.bfloat16)
    wide_feats = features.astype(jnp.float32)
    row_norm = jnp.sqrt(jnp.sum(wide_feats * wide_feats, axis=1, keepdims=True) + epsilon)
    unit_rows = (wide_feats / row_norm).astype(jnp.bfloat16)
    images = features.shape[0] * lax.axis_size("dp")
    logits = jnp.dot(
        lax.all_gather(unit_rows, "dp", axis=0, tiled=True),
        protos,
        preferred_element_type=jnp.float32,
    )
    column_sums = jnp.sum(logits, axis=0)
    new_center = center_momentum * center + (1.0 - center_momentum) * (column_sums / images)
    shifted = (logits - new_center[None, :]) / teacher_temp
    totals = lax.psum(jnp.sum(jnp.exp(shifted), axis=1), ("dp", "mp"))
    log_targets = shifted - jnp.log(totals)[:, None]
    return (blended, new_center, log_targets)


def solution(mesh):
    placed = (P("dp", None), P(None, ("dp", "mp")), P(None, ("dp", "mp")), P(("dp", "mp")))
    return jax.shard_map(
        shards,
        mesh=mesh,
        in_specs=placed,
        out_specs=(P(None, ("dp", "mp")), P(("dp", "mp")), P(None, ("dp", "mp"))),
        check_vma=False,
    )
```

profile of v0, /device:TPU:10, one launch (start us, length us, event | category | flops | bytes accessed | tf_op | source)
XLA Modules:
  0.0 98.9 jit_solution(8793507337813024451)
XLA Ops:
  0.6 0.9 fusion.3
  1.5 0.9 fusion.4
  2.4 20.6 %all_gather.3 = bf16[768,384]{1,0:T(8,128)(2,1)S(1)} all-gather(bf16[48,384]{1,0:T(8,128)(2,1)S(1)} %fusion.4), channel_id=1, replica_groups=mesh['dp'=16,'mp'=2] {'dp'}, dimensions={0}, use_global_device_ids=true | all-gather | bytes 626688 | tf_op jit(solution)/shard_map/all_gather | solution.py:21
  22.9 9.3 %multiply_reduce_fusion = (f32[4096]{0:T(1024)S(1)}, f32[384,4096]{1,0:T(8,128)}) fusion(f32[384,4096]{1,0:T(8,128)} %param.6, f32[384,4096]{1,0:T(8,128)} %param.5), kind=kLoop, calls=%fused_computation.4 | loop fusion | flops 7860224 | bytes 18890752 | tf_op jit(solution)/shard_map/reduce_sum | solution.py:14
  32.3 0.0 copy-start.2
  32.3 5.6 %fusion.5 = (f32[4096]{0:T(1024)S(1)}, f32[768,4096]{1,0:T(8,128)S(1)}) fusion(bf16[768,384]{1,0:T(8,128)(2,1)S(1)} %all_gather.3, f32[384,4096]{1,0:T(8,128)} %get-tuple-element.4, f32[4096]{0:T(1024)S(1)} %add_sqrt_fusion), kind=kOutput, calls=%fused_computation.15 | convolution fusion | flops 2422206464 | bytes 19496960 | tf_op jit(solution)/shard_map/dot_general | solution.py:20
  37.9 0.0 copy-start
  37.9 0.0 copy-done.2
  37.9 4.7 %copy-done = f32[768,4096]{1,0:T(8,128)} copy-done((f32[768,4096]{1,0:T(8,128)}, f32[768,4096]{1,0:T(8,128)S(1)}, u32[]{:S(2)}) %copy-start) | copy-done | bytes 12582936
  42.7 0.0 copy-start.1
  42.7 2.2 %exponential_reduce_fusion = f32[768]{0:T(1024)S(1)} fusion(f32[768,4096]{1,0:T(8,128)S(1)} %get-tuple-element.6, f32[4096]{0:T(1024)S(1)} %multiply_add_fusion.1), kind=kLoop, calls=%fused_computation | loop fusion | flops 9436416 | bytes 12602368 | tf_op jit(solution)/shard_map/reduce_sum | solution.py:28
  44.9 41.8 %psum.7 = f32[768]{0:T(1024)S(1)} all-reduce(f32[768]{0:T(1024)S(1)} %exponential_reduce_fusion), channel_id=1, replica_groups=mesh['dp'=16,'mp'=2] {'dp','mp'}, use_global_device_ids=true, to_apply=%region_4.0 | all-reduce | flops 768 | bytes 6144 | tf_op jit(solution)/shard_map/psum | solution.py:28
  86.6 0.0 copy-done.1
  86.6 12.2 %fusion = f32[768,4096]{1,0:T(8,128)} fusion(f32[768,4096]{1,0:T(8,128)} %copy-done, f32[768]{0:T(1024)S(1)} %log.3, f32[4096]{0:T(1024)S(1)} %multiply_add_fusion.1), kind=kLoop, calls=%fused_computation.2 | loop fusion | flops 9437184 | bytes 25185280 | tf_op jit(solution)/shard_map/sub | solution.py:29
  (4 shorter events, 0.0 us)
Async XLA Ops:
  32.3 5.6 %copy-start.2 = (f32[4096]{0:T(1024)S(1)}, f32[4096]{0:T(1024)}, u32[]{:S(2)}) copy-start(f32[4096]{0:T(1024)} %param.7) | copy-start | bytes 49156
  37.9 4.8 %copy-start = (f32[768,4096]{1,0:T(8,128)}, f32[768,4096]{1,0:T(8,128)S(1)}, u32[]{:S(2)}) copy-start(f32[768,4096]{1,0:T(8,128)S(1)} %get-tuple-element.6) | copy-start | bytes 37748740
  42.7 44.0 %copy-start.1 = (f32[4096]{0:T(1024)}, f32[4096]{0:T(1024)S(1)}, u32[]{:S(2)}) copy-start(f32[4096]{0:T(1024)S(1)} %multiply_add_fusion.1) | copy-start | bytes 49156
where the time goes:
time: 99.2 us; the launch traced here: 98.9 us
  blocking collectives  62.3 us (63%)
  other arithmetic  25.5 us (26%)
  matrix products  5.6 us (6%)
  local copies, waits for them, and re-layouts  4.76 us (5%)
    psum x1, blocking collectives, shards(): totals = lax.psum(jnp.sum(jnp.exp(shifted), axis=1), ('dp', 'mp'))  41.8 us
    all_gather x1, blocking collectives, shards(): lax.all_gather(unit_rows, 'dp', axis=0, tiled=True)  20.6 us
    sub x1, other arithmetic, shards(): log_targets = shifted - jnp.log(totals)[:, None]  12.2 us
    reduce_sum x1, other arithmetic, shards(): jnp.sum(blended * blended, axis=0, keepdims=True) + epsilon  9.32 us
    dot_general x1, matrix products, shards(): jnp.dot(lax.all_gather(unit_rows, 'dp', axis=0, tiled=True), protos, pref...  5.6 us
    unnamed x6, local copies, waits for them, and re-layouts  4.76 us
    reduce_sum x1, other arithmetic, shards(): totals = lax.psum(jnp.sum(jnp.exp(shifted), axis=1), ('dp', 'mp'))  2.18 us

commit v1 on v0

--- a/solution.py
+++ b/solution.py
@@ -25,7 +25,7 @@
     column_sums = jnp.sum(logits, axis=0)
     new_center = center_momentum * center + (1.0 - center_momentum) * (column_sums / images)
     shifted = (logits - new_center[None, :]) / teacher_temp
-    totals = lax.psum(jnp.sum(jnp.exp(shifted), axis=1), ("dp", "mp"))
+    totals = jnp.sum(lax.all_gather(jnp.sum(jnp.exp(shifted), axis=1), ("dp", "mp")), axis=0)
     log_targets = shifted - jnp.log(totals)[:, None]
     return (blended, new_center, log_targets)
 

time: 99.2 us -> 125 us (1.26)
  the two profiles are of different devices: /device:TPU:10 before, /device:TPU:0 now
where the time goes in v1:
time: 125 us
  blocking collectives  90.1 us (72%)
  other arithmetic  25.6 us (20%)
  matrix products  5.6 us (4%)
  local copies, waits for them, and re-layouts  2.57 us (2%)
    all_gather x1, blocking collectives, shards(): lax.all_gather(jnp.sum(jnp.exp(shifted), axis=1), ('dp', 'mp'))  65.3 us
    all_gather x1, blocking collectives, shards(): lax.all_gather(unit_rows, 'dp', axis=0, tiled=True)  24.9 us
    sub x1, other arithmetic, shards(): log_targets = shifted - jnp.log(totals)[:, None]  12.2 us
    reduce_sum x1, other arithmetic, shards(): jnp.sum(blended * blended, axis=0, keepdims=True) + epsilon  9.32 us
    dot_general x1, matrix products, shards(): jnp.dot(lax.all_gather(unit_rows, 'dp', axis=0, tiled=True), protos, pref...  5.6 us
    unnamed x7, local copies, waits for them, and re-layouts  2.57 us

profile of v1, /device:TPU:0, one launch (start us, length us, event | category | flops | bytes accessed | tf_op | source)
XLA Modules:
  0.0 124.6 jit_solution(4416093036752738489)
XLA Ops:
  0.6 0.9 fusion.3
  1.5 0.9 fusion.4
  2.4 24.9 %all_gather.9 = bf16[768,384]{1,0:T(8,128)(2,1)S(1)} all-gather(bf16[48,384]{1,0:T(8,128)(2,1)S(1)} %fusion.4), channel_id=1, replica_groups=mesh['dp'=16,'mp'=2] {'dp'}, dimensions={0}, use_global_device_ids=true | all-gather | bytes 626688 | tf_op jit(solution)/shard_map/all_gather | solution.py:21
  27.3 9.3 %multiply_reduce_fusion = (f32[4096]{0:T(1024)S(1)}, f32[384,4096]{1,0:T(8,128)}) fusion(f32[384,4096]{1,0:T(8,128)} %param.6, f32[384,4096]{1,0:T(8,128)} %param.5), kind=kLoop, calls=%fused_computation.4 | loop fusion | flops 7860224 | bytes 18890752 | tf_op jit(solution)/shard_map/reduce_sum | solution.py:14
  36.6 0.0 copy-start.2
  36.6 5.6 %fusion.5 = (f32[4096]{0:T(1024)S(1)}, f32[768,4096]{1,0:T(8,128)S(1)}) fusion(bf16[768,384]{1,0:T(8,128)(2,1)S(1)} %all_gather.9, f32[384,4096]{1,0:T(8,128)} %get-tuple-element.4, f32[4096]{0:T(1024)S(1)} %add_sqrt_fusion), kind=kOutput, calls=%fused_computation.15 | convolution fusion | flops 2422206464 | bytes 19496960 | tf_op jit(solution)/shard_map/dot_general | solution.py:20
  42.2 0.0 copy-start
  42.2 0.0 copy-done.2
  42.3 0.0 copy-start.1
  42.3 2.2 %exponential_reduce_fusion = f32[768]{0:T(1024)S(1)} fusion(f32[768,4096]{1,0:T(8,128)S(1)} %get-tuple-element.6, f32[4096]{0:T(1024)S(1)} %multiply_add_fusion.1), kind=kLoop, calls=%fused_computation | loop fusion | flops 9436416 | bytes 12602368 | tf_op jit(solution)/shard_map/reduce_sum | solution.py:28
  44.5 2.5 %copy-done = f32[768,4096]{1,0:T(8,128)} copy-done((f32[768,4096]{1,0:T(8,128)}, f32[768,4096]{1,0:T(8,128)S(1)}, u32[]{:S(2)}) %copy-start) | copy-done | bytes 12582936
  47.0 65.3 %all-gather.1 = f32[32,1,768]{2,1,0:T(1,128)S(1)} all-gather(f32[1,1,768]{2,1,0:T(1,128)S(1)} %reshape.23), channel_id=2, replica_groups=mesh['dp'=16,'mp'=2] {'dp','mp'}, dimensions={0}, use_global_device_ids=true | all-gather | bytes 101376 | tf_op jit(solution)/shard_map/all_gather | solution.py:28
  112.3 0.1 reduce_sum.49
  112.4 0.0 copy-done.1
  112.4 12.2 %fusion = f32[768,4096]{1,0:T(8,128)} fusion(f32[768,4096]{1,0:T(8,128)} %copy-done, f32[768]{0:T(1024)S(1)} %log.7, f32[4096]{0:T(1024)S(1)} %multiply_add_fusion.1), kind=kLoop, calls=%fused_computation.2 | loop fusion | flops 9437184 | bytes 25185280 | tf_op jit(solution)/shard_map/sub | solution.py:29
  (5 shorter events, 0.0 us)
Async XLA Ops:
  36.6 5.6 %copy-start.2 = (f32[4096]{0:T(1024)S(1)}, f32[4096]{0:T(1024)}, u32[]{:S(2)}) copy-start(f32[4096]{0:T(1024)} %param.7) | copy-start | bytes 49156
  42.2 4.8 %copy-start = (f32[768,4096]{1,0:T(8,128)}, f32[768,4096]{1,0:T(8,128)S(1)}, u32[]{:S(2)}) copy-start(f32[768,4096]{1,0:T(8,128)S(1)} %get-tuple-element.6) | copy-start | bytes 37748740
  42.3 70.1 %copy-start.1 = (f32[4096]{0:T(1024)}, f32[4096]{0:T(1024)S(1)}, u32[]{:S(2)}) copy-start(f32[4096]{0:T(1024)S(1)} %multiply_add_fusion.1) | copy-start | bytes 49156
